TPU v7x, 32 devices: a whole 2x2x4 slice. The times are simulated.
32 devices in a mesh: img: 4 (over x, core), patch: 8 (over z, y).
Axes of the slice: x: 2, y: 2, z: 4, core: 2. Of those that a mesh axis runs over, the one named last changes fastest.
Arguments:
- hidden: bfloat16 [8, 8, 128, 640], P('img', 'patch'), may hold values from -100 to 100
- stale_attn_in: bfloat16 [8, 8, 128, 640], P('img', 'patch'), may hold values from -100 to 100
- stale_conv_in: bfloat16 [8, 8, 128, 640], P('img', 'patch'), may hold values from -6 to 6
- ln_gain: float32 [640], replicated, may hold values from 0.25 to 1.75
- ln_bias: float32 [640], replicated, may hold values from -2 to 2
- w_qkv: bfloat16 [640, 1920], replicated, may hold values from -3 to 3
- w_out: bfloat16 [640, 640], replicated, may hold values from -0.25 to 0.25
- gn_gain: float32 [640], replicated, may hold values from 0.25 to 1.75
- gn_bias: float32 [640], replicated, may hold values from -1.5 to 1.5
- conv_weight: bfloat16 [3, 3, 640, 640], replicated, may hold values from -0.078125 to 0.078125
- conv_bias: float32 [640], replicated, may hold values from -1.5 to 1.5
- time_shift: float32 [8, 640], P('img'), may hold values from -6 to 6
Outputs:
- block_out: bfloat16 [8, 8, 128, 640], P('img', 'patch')
All inputs are finite; a program needn't handle non-finite values.
Results may differ from a plain program's by a relative error of at most 0.0075.
The roundings to bfloat16 on the way count: a program that leaves them out, or rounds other values in their place, can miss the bound.
Values may be sent and summed in bfloat16 or wider, within the bound.
A program may use at most 128 MiB of HBM per device.

v0:
```python
import functools

import jax
import jax.numpy as jnp
from jax import lax
from jax.experimental import pallas as pl
from jax.experimental.pallas import tpu as pltpu
from jax.sharding import PartitionSpec as P

GROUPS = 32
HEAD_DIM = 64
EPSILON = 1e-05
PARTS = 2
EDGE_STEP = 0
PASS_STEP = 2
MESH = pl.DeviceIdType.MESH
F32 = jnp.float32
BF16 = jnp.bfloat16


def layer_norm(values, gain, bias):
    values = values.astype(F32)
    centre = jnp.mean(values, -1, keepdims=True)
    centred = values - centre
    spread = jnp.mean(centred * centred, -1, keepdims=True)
    return (centred * lax.rsqrt(spread + EPSILON) * gain + bias).astype(BF16)


def dot(a, b):
    return jnp.dot(a, b, preferred_element_type=F32)


def split_dot(a, b):
    high = a.astype(BF16)
    rest = a - high.astype(F32)
    mid = rest.astype(BF16)
    low = (rest - mid.astype(F32)).astype(BF16)
    return dot(high, b) + dot(mid, b) + dot(low, b)


def kernel(
    n,
    hidden,
    stale_attn,
    stale_conv,
    ln_gain_hbm,
    ln_bias_hbm,
    w_qkv_hbm,
    w_out_hbm,
    gn_gain_hbm,
    gn_bias_hbm,
    conv_w_hbm,
    conv_bias_hbm,
    time_shift,
    out,
    ln_gain,
    ln_bias,
    gn_gain,
    gn_bias,
    conv_bias,
    vector_sem,
    w_qkv,
    w_out,
    conv_w,
    blocks,
    edges,
    w_vt,
    q_diag,
    maxima,
    sums,
    accum,
    same_group,
    conv_acc,
    stats,
    weight_sem,
    gather_send,
    gather_recv,
    edge_send,
    edge_recv,
    stat_send,
    stat_recv,
):
    samples, _, cols, channels = hidden.shape
    tokens = samples * cols
    pairs = channels // (2 * HEAD_DIM)
    wide = 2 * cols
    group_size = channels // GROUPS
    side = 2
    length = n // side
    me = lax.axis_index("patch")
    z = me // side
    y = me % side

    load_qkv = pltpu.make_async_copy(w_qkv_hbm, w_qkv, weight_sem.at[0])
    load_out = pltpu.make_async_copy(w_out_hbm, w_out, weight_sem.at[1])
    load_conv = pltpu.make_async_copy(conv_w_hbm, conv_w, weight_sem.at[2])
    vectors = [
        pltpu.make_async_copy(source, target, vector_sem.at[i])
        for i, (source, target) in enumerate(
            (
                (ln_gain_hbm, ln_gain),
                (ln_bias_hbm, ln_bias),
                (gn_gain_hbm, gn_gain),
                (gn_bias_hbm, gn_bias),
                (conv_bias_hbm, conv_bias),
            )
        )
    ]
    for load in vectors:
        load.start()
    load_qkv.start()
    load_out.start()
    load_conv.start()

    barrier = pltpu.get_barrier_semaphore()
    for step in range(1, n):
        pl.semaphore_signal(
            barrier, inc=1, device_id={"patch": lax.rem(me + step, n)}, device_id_type=MESH
        )
    for load in vectors:
        load.wait()
    parts = blocks.shape[1]
    normed = layer_norm(stale_attn[:, 0], ln_gain[...], ln_bias[...])
    blocks[me] = normed.reshape(parts, tokens // parts, channels)
    pl.semaphore_wait(barrier, n - 1)

    def block_copy(way, source, part, target):
        return pltpu.make_async_remote_copy(
            src_ref=blocks.at[source, part],
            dst_ref=blocks.at[source, part],
            send_sem=gather_send.at[way, source, part],
            recv_sem=gather_recv.at[source, part],
            device_id={"patch": target},
            device_id_type=MESH,
        )

    def spread(source_z, source_y, part, act):
        source = source_z * side + source_y
        late = part >= parts // 2
        own_column = source_y == y
        gap = jnp.abs(source_z - z)
        at_end = (z == 0) | (z == length - 1)
        across = own_column & ((gap != 1) if late else ((gap != 1) | at_end))
        pl.when(across)(lambda: act(block_copy(2, source, part, z * side + (1 - y))))
        up = own_column & (source_z <= z) & (z < length - 1)
        down = own_column & (source_z >= z) & (z > 0)
        pl.when(up)(lambda: act(block_copy(0, source, part, me + side)))
        pl.when(down)(lambda: act(block_copy(1, source, part, me - side)))
        beside = (source_y != y) & (gap == 0)
        turn_up = beside & (z < (length - 1 if late else length - 2))
        turn_down = beside & (z > (0 if late else 1))
        pl.when(turn_up)(lambda: act(block_copy(3, source, part, me + side)))
        pl.when(turn_down)(lambda: act(block_copy(4, source, part, me - side)))

    def arrival(k):
        j = (k + 1) // 2
        other = 1 - (k % 2)
        near = jnp.minimum(z, length - 1 - z)
        toward = jnp.where(z * 2 < length, 1, -1)
        both = j <= 2 * near
        step = jnp.where(both, (j + 1) // 2, j - near)
        sign = jnp.where(both, jnp.where(j % 2 == 1, toward, -toward), toward)
        return z + jnp.where(j == 0, 0, step * sign), jnp.where(other == 1, 1 - y, y)

    for part in range(parts):
        spread(z, y, part, lambda copy: copy.start())

    def edge_copy(hop):
        return pltpu.make_async_remote_copy(
            src_ref=stale_conv.at[:, 0] if hop == 0 else edges.at[1 - y],
            dst_ref=edges.at[y],
            send_sem=edge_send.at[hop],
            recv_sem=edge_recv.at[y],
            device_id={"patch": z * side + (1 - y) if hop == 0 else me + side * (1 - 2 * y)},
            device_id_type=MESH,
        )

    def edge_wait(slot):
        pltpu.make_async_remote_copy(
            src_ref=edges.at[slot],
            dst_ref=edges.at[slot],
            send_sem=edge_send.at[0],
            recv_sem=edge_recv.at[slot],
            device_id={"patch": z * side + (1 - y)},
            device_id_type=MESH,
        ).wait_recv()

    below_exists = z < length - 1
    above_exists = z > 0
    hands_on = ((y == 0) & below_exists) | ((y == 1) & above_exists)
    is_handed = ((y == 0) & above_exists) | ((y == 1) & below_exists)

    fresh = layer_norm(hidden[:, 0], ln_gain[...], ln_bias[...]).reshape(tokens, channels)
    load_qkv.wait()
    queries = dot(fresh, w_qkv[:, :channels]).astype(BF16).astype(F32) * HEAD_DIM ** (-0.5)
    q_t = queries.T.astype(BF16)
    q_diag[...] = jnp.zeros_like(q_diag)
    for sample in range(samples):
        for pair in range(pairs):
            for half in range(2):
                row = (2 * pair + half) * HEAD_DIM
                q_diag[
                    sample, pair, half * HEAD_DIM : (half + 1) * HEAD_DIM, half * cols : (half + 1) * cols
                ] = q_t[row : row + HEAD_DIM, sample * cols : (sample + 1) * cols]
    w_vt[...] = w_qkv[:, 2 * channels :].astype(F32).T.astype(BF16)
    channel_row = lax.broadcasted_iota(jnp.int32, (channels, channels), 0) // group_size
    channel_col = lax.broadcasted_iota(jnp.int32, (channels, channels), 1) // group_size
    same_group[...] = jnp.where(channel_row == channel_col, 1.0, 0.0).astype(BF16)

    def absorb(groups, first):
        rows = jnp.concatenate([g[s] for s in range(samples) for g in groups], 0)
        width = len(groups) * cols
        keys = dot(rows, w_qkv[:, channels : 2 * channels]).astype(BF16)
        values_t = lax.dot_general(
            w_vt[...], rows, (((1,), (1,)), ((), ())), preferred_element_type=F32
        ).astype(BF16)
        for sample in range(samples):
            span = slice(sample * width, (sample + 1) * width)
            for pair in range(pairs):
                scores = dot(
                    keys[span, pair * 2 * HEAD_DIM : (pair + 1) * 2 * HEAD_DIM], q_diag[sample, pair]
                )
                new_max = jnp.max(scores, 0, keepdims=True)
                if not first:
                    old_max = maxima[sample, pair : pair + 1]
                    new_max = jnp.maximum(old_max, new_max)
                    rescale = jnp.exp(old_max - new_max)
                weights = jnp.exp(scores - new_max)
                total = jnp.sum(weights, 0, keepdims=True)
                if not first:
                    total = total + sums[sample, pair : pair + 1] * rescale
                maxima[sample, pair : pair + 1] = new_max
                sums[sample, pair : pair + 1] = total
                weights = weights.astype(BF16)
                for half in range(2):
                    row = (2 * pair + half) * HEAD_DIM
                    lanes = slice(half * cols, (half + 1) * cols)
                    part = dot(values_t[row : row + HEAD_DIM, span], weights[:, lanes])
                    if not first:
                        part = part + accum[sample, row : row + HEAD_DIM] * rescale[:, lanes]
                    accum[sample, row : row + HEAD_DIM] = part

    absorb([fresh.reshape(samples, cols, channels)], True)

    def receive(k):
        source_z, source_y = arrival(k)
        source = source_z * side + source_y
        for part in range(parts):
            block_copy(0, source, part, source).wait_recv()
            spread(source_z, source_y, part, lambda copy: copy.start())
        return source

    def block(source):
        return blocks[source].reshape(samples, cols, channels)

    def pass_edges():
        edge_wait(1 - y)
        pl.when(hands_on)(lambda: edge_copy(1).start())

    def step(j, carry):
        first, second = receive(2 * j), receive(2 * j + 1)
        pl.when(j == EDGE_STEP)(lambda: edge_copy(0).start())
        pl.when(j == PASS_STEP)(pass_edges)
        absorb([block(first), block(second)], False)
        return carry

    lax.fori_loop(0, (n - 1) // 2, step, 0)
    if (n - 1) % 2 == 1:
        absorb([block(receive(n - 2))], False)

    for sample in range(samples):
        for head in range(2 * pairs):
            row = head * HEAD_DIM
            total = sums[sample, head // 2 : head // 2 + 1, (head % 2) * cols : (head % 2 + 1) * cols]
            accum[sample, row : row + HEAD_DIM] = accum[sample, row : row + HEAD_DIM] / total
    attended = jnp.concatenate([accum[s].T for s in range(samples)], 0).astype(BF16)
    load_out.wait()
    residual = hidden[:, 0].reshape(tokens, channels).astype(F32) + dot(attended, w_out[...])
    residual = residual.astype(BF16).astype(F32).reshape(samples, cols, channels)

    sum_rows = jnp.concatenate([jnp.sum(residual[s], 0, keepdims=True) for s in range(samples)], 0)
    cells = cols * group_size
    local_mean = split_dot(sum_rows, same_group[...]) / cells
    centred = residual - local_mean[:, None, :]
    square_rows = jnp.concatenate(
        [jnp.sum(centred[s] * centred[s], 0, keepdims=True) for s in range(samples)], 0
    )
    local_square = split_dot(square_rows, same_group[...])
    stats[me, :samples] = local_mean
    stats[me, samples:] = local_square

    def stat_copy(distance):
        return pltpu.make_async_remote_copy(
            src_ref=stats.at[me],
            dst_ref=stats.at[me],
            send_sem=stat_send.at[distance],
            recv_sem=stat_recv.at[me],
            device_id={"patch": lax.rem(me + distance, n)},
            device_id_type=MESH,
        )

    for distance in range(1, n):
        stat_copy(distance).start()

    @pl.when(me == 0)
    def _():
        edges[0] = jnp.zeros_like(edges[0])

    @pl.when(me == n - 1)
    def _():
        edges[1] = jnp.zeros_like(edges[1])

    pl.when(is_handed)(lambda: edge_wait(y))
    load_conv.wait()
    above = edges[0].reshape(tokens, channels)
    below = edges[1].reshape(tokens, channels)
    for tap in range(3):
        conv_acc[tap] = dot(above, conv_w[0, tap]) + dot(below, conv_w[2, tap])

    for distance in range(1, n):
        source = lax.rem(me + distance, n)
        pltpu.make_async_remote_copy(
            src_ref=stats.at[source],
            dst_ref=stats.at[source],
            send_sem=stat_send.at[distance],
            recv_sem=stat_recv.at[source],
            device_id={"patch": source},
            device_id_type=MESH,
        ).wait_recv()
    every = stats[...]
    group_mean = jnp.mean(every[:, :samples], 0)
    shift = every[:, :samples] - group_mean[None]
    group_var = (jnp.sum(every[:, samples:], 0) + cells * jnp.sum(shift * shift, 0)) / (cells * n)
    scale = lax.rsqrt(group_var + EPSILON)
    pre = (residual - group_mean[:, None, :]) * scale[:, None, :] * gn_gain[...] + gn_bias[...]
    activated = (pre / (1.0 + jnp.exp(-pre))).astype(BF16).reshape(tokens, channels)

    column = lax.broadcasted_iota(jnp.int32, (tokens, 1), 0) % cols
    total = conv_acc[1] + dot(activated, conv_w[1, 1])
    left = pltpu.roll(conv_acc[0] + dot(activated, conv_w[1, 0]), 1, 0)
    total = total + jnp.where(column == 0, 0.0, left)
    right = pltpu.roll(conv_acc[2] + dot(activated, conv_w[1, 2]), tokens - 1, 0)
    total = total + jnp.where(column == cols - 1, 0.0, right)
    total = total.reshape(samples, cols, channels) + conv_bias[...]
    for sample in range(samples):
        out[sample, 0] = (
            total[sample] + time_shift[sample : sample + 1] + residual[sample]
        ).astype(BF16)

    for part in range(parts):
        spread(z, y, part, lambda copy: copy.wait_send())

    def drain(k, carry):
        source_z, source_y = arrival(k)
        for part in range(parts):
            spread(source_z, source_y, part, lambda copy: copy.wait_send())
        return carry

    lax.fori_loop(0, n - 1, drain, 0)
    edge_copy(0).wait_send()
    pl.when(hands_on)(lambda: edge_copy(1).wait_send())
    for distance in range(1, n):
        stat_copy(distance).wait_send()


def shards(n, *arrays):
    (hidden, stale_attn, stale_conv, ln_gain, ln_bias, w_qkv, w_out) = arrays[:7]
    (gn_gain, gn_bias, conv_w, conv_bias, time_shift) = arrays[7:]
    samples, rows_dev, cols, channels = hidden.shape
    assert rows_dev == 1 and n % 2 == 0, "unsupported split"
    tokens = samples * cols
    parts = PARTS * samples
    pairs = channels // (2 * HEAD_DIM)
    vmem = pl.BlockSpec(memory_space=pltpu.VMEM)
    hbm = pl.BlockSpec(memory_space=pl.ANY)
    dma = pltpu.SemaphoreType.DMA
    return pl.pallas_call(
        functools.partial(kernel, n),
        out_shape=jax.ShapeDtypeStruct(hidden.shape, BF16),
        in_specs=[vmem] * 3 + [hbm] * 8 + [vmem],
        out_specs=vmem,
        scratch_shapes=[pltpu.VMEM((channels,), F32)] * 5
        + [
            dma((5,)),
            pltpu.VMEM(w_qkv.shape, BF16),
            pltpu.VMEM(w_out.shape, BF16),
            pltpu.VMEM(conv_w.shape, BF16),
            pltpu.VMEM((n, parts, tokens // parts, channels), BF16),
            pltpu.VMEM((2, samples, cols, channels), BF16),
            pltpu.VMEM((channels, channels), BF16),
            pltpu.VMEM((samples, pairs, 2 * HEAD_DIM, 2 * cols), BF16),
            pltpu.VMEM((samples, pairs, 2 * cols), F32),
            pltpu.VMEM((samples, pairs, 2 * cols), F32),
            pltpu.VMEM((samples, channels, cols), F32),
            pltpu.VMEM((channels, channels), BF16),
            pltpu.VMEM((3, tokens, channels), F32),
            pltpu.VMEM((n, 2 * samples, channels), F32),
            dma((3,)),
            dma((5, n, parts)),
            dma((n, parts)),
            dma((2,)),
            dma((2,)),
            dma((n,)),
            dma((n,)),
        ],
        compiler_params=pltpu.CompilerParams(
            collective_id=0, has_side_effects=True, vmem_limit_bytes=56 * 2**20
        ),
        name="section",
    )(
        hidden,
        stale_attn,
        stale_conv,
        ln_gain,
        ln_bias,
        w_qkv,
        w_out,
        gn_gain,
        gn_bias,
        conv_w,
        conv_bias,
        time_shift,
    )


def solution(mesh):
    wide = P("img", "patch", None, None)
    in_specs = (wide, wide, wide) + (P(),) * 8 + (P("img", None),)
    body = functools.partial(shards, mesh.shape["patch"])
    return jax.shard_map(body, mesh=mesh, in_specs=in_specs, out_specs=wide, check_vma=False)
```

profile of v0, /device:TPU:0, one launch (start us, length us, event | category | flops | bytes accessed | tf_op | source)
XLA Modules:
  0.0 55.9 jit_solution(6694402727472660752)
XLA Ops:
  0.0 54.1 %section.1 = bf16[2,1,128,640]{3,2,1,0:T(8,128)(2,1)} custom-call(bf16[2,1,128,640]{3,2,1,0:T(8,128)(2,1)} %hidden.1, bf16[2,1,128,640]{3,2,1,0:T(8,128)(2,1)} %stale_attn.1, bf16[2,1,128,640]{3,2,1,0:T(8,128)(2,1)} %stale_conv.1, f32[640]{0:T(1024)} %ln_gain_hbm.1, f32[640]{0:T(1024)} %ln_bias_hbm.1, bf16[640,1920]{1,0:T(8,128)(2,1)} %w_qkv_hbm.1, ...), custom_call_target="tpu_custom_call" | custom-call | tf_op jit(solution)/shard_map/section/pallas_call | solution.py:377
  54.1 1.7 %copy.14 = bf16[2,1,128,640]{3,2,1,0:T(8,128)(2,1)} copy(bf16[2,1,128,640]{3,2,1,0:T(8,128)(2,1)} %section.1) | data formatting | bytes 655360
where the time goes:
time: 56 us; the launch traced here: 55.9 us
  Pallas kernels  54.1 us (97%)
  local copies, waits for them, and re-layouts  1.73 us (3%)
    pallas_call x1, Pallas kernels, shards(): pl.pallas_call(functools.partial(kernel, n), out_shape=jax.ShapeDtypeStru...  54.1 us
    unnamed x1, local copies, waits for them, and re-layouts  1.73 us

commit v1 on v0

v1 whole, which is shorter than its diff:
```python
import functools
import heapq
import itertools

import jax
import jax.numpy as jnp
from jax import lax
from jax.experimental import pallas as pl
from jax.experimental.pallas import tpu as pltpu
from jax.sharding import PartitionSpec as P

GROUPS = 32
HEAD_DIM = 64
EPSILON = 1e-05
MESH = pl.DeviceIdType.MESH
F32 = jnp.float32
BF16 = jnp.bfloat16

DOWN, UP, ACROSS = 0, 1, 2
MOVED = True
TUNED = {
    4: [
        (
            [6, 22, 770, 786, 612, 38, 88, 140, 122, 152, 54, 580, 74, 188, 248, 316, 200, 216, 300, 682, 628, 232, 666, 596, 106, 168, 360, 376, 444, 698, 428, 650, 488, 984, 504, 968],
            35,
            36,
            [(0, 0, 0), (0, 1, 0), (1, 0, 0), (1, 1, 0), (1, 2, 0), (1, 3, 0)],
            [13, 18, 25, 26, 28, 35],
        ),
        (
            [135, 151, 167, 596, 183, 580, 10, 219, 313, 30, 200, 280, 235, 297, 840, 42, 268, 328, 88, 120, 412, 58, 360, 650, 628, 72, 396, 456, 445, 472, 856, 250, 429, 744, 344, 698, 728, 612, 104, 488, 376, 666, 682, 760, 504, 712],
            45,
            45,
            [(0, 1, 0), (0, 0, 0), (0, 3, 3), (0, 2, 5), (1, 1, 0), (1, 0, 0), (1, 2, 0), (1, 3, 0)],
            [11, 26, 31, 35, 35, 39, 41, 45],
        ),
        (
            [263, 279, 311, 295, 140, 363, 393, 170, 413, 666, 580, 186, 328, 425, 12, 456, 650, 28, 441, 472, 216, 347, 488, 628, 152, 200, 840, 46, 88, 856, 596, 232, 377, 612, 62, 698, 72, 712, 104, 248, 120, 760, 682, 504, 728, 744],
            44,
            44,
            [(0, 3, 0), (0, 2, 0), (0, 1, 3), (0, 0, 5), (1, 2, 0), (1, 1, 0), (1, 0, 0), (1, 3, 0)],
            [20, 22, 30, 37, 37, 40, 41, 44],
        ),
        (
            [389, 405, 769, 785, 437, 421, 316, 457, 268, 680, 612, 296, 489, 596, 328, 360, 472, 728, 172, 648, 188, 248, 628, 376, 712, 580, 232, 344, 280, 696, 44, 664, 505, 60, 120, 760, 104, 968, 984, 744],
            37,
            39,
            [(0, 3, 0), (0, 2, 0), (1, 2, 0), (1, 1, 0), (1, 3, 0), (1, 0, 0)],
            [17, 29, 29, 29, 33, 37],
        ),
    ]
}


def special_parts(length):
    return tuple(8 * length + 4 * k for k in range(1, 8))


def mirrored_part(length, y, part):
    return part if y == 0 or part >= 8 * length else 4 * (2 * length - 1 - part // 4) + part % 4


def transfers(length):
    own_edge, cross, handed, q_own, q_far, o_own, o_far = special_parts(length)
    ends = (0, length - 1)

    def turned(zd, sz, half):
        return abs(sz - zd) == 1 and (half == 1 or (zd not in ends and sz in ends))

    result = {}
    for z, y in itertools.product(range(length), range(2)):
        sends = {}
        sides = [(k, zd) for k, zd in ((DOWN, z - 1), (UP, z + 1)) if 0 <= zd < length]
        for sz, sy, sp in itertools.product(range(length), range(2), range(4)):
            part = (2 * sz + sy) * 4 + sp
            sends[part] = [
                (k, part)
                for k, zd in sides
                if needs(length, zd, sz, sp // 2)
                and ((sz <= z if k == UP else sz >= z) if sy == y else sz == z and turned(zd, sz, sp % 2))
            ]
            if sy == y and needs(length, z, sz, sp // 2) and not turned(z, sz, sp % 2):
                sends[part].append((ACROSS, part))
        on = UP if y == 0 else DOWN
        for k in range(4):
            sends[own_edge + k] = [(ACROSS, cross + k)]
            sends[cross + k] = [(on, handed + k)] if on in dict(sides) else []
        for k in range(2):
            sends[q_own + k] = [(UP if z == 0 else DOWN, q_far + k)] if z in ends else []
            sends[o_own + k] = [(DOWN if z == 1 else UP, o_far + k)] if z in (1, length - 2) else []
        result[z, y] = sends
    return result


def needs(length, z, sz, sample):
    return not (sample == 0 and z in (0, length - 1) and abs(sz - z) > 1)


def programs_by_time(length):
    own_edge, cross, handed, q_own, q_far, o_own, o_far = special_parts(length)
    ends = (0, length - 1)
    sends = transfers(length)
    queues, busy, events, count = {}, {}, [], itertools.count()
    landed = {d: {} for d in sends}
    left, answered = {}, set()
    rank = {own_edge: 5, cross: 4, handed: 4, q_own: 0, q_far: 0, o_own: -1, o_far: -1}

    def push(t, kind, *rest):
        heapq.heappush(events, (t, next(count), kind, rest))

    def offer(t, d, part):
        for k, there in sends[d].get(part, []):
            push(t, "queue", d, k, part, there)

    def launch(t, d, k):
        busy[d, k] = bool(queues[d, k])
        if busy[d, k]:
            _, there, part = heapq.heappop(queues[d, k])
            left.setdefault((d, part), t)
            push(t + 1.76, "sent", d, k, there)

    for d in sends:
        for k in range(4):
            offer(0.0, d, (2 * d[0] + d[1]) * 4 + k)
            offer(0.0, d, own_edge + k)
        for k in range(2):
            if d[0] in ends:
                offer(2.0, d, q_own + k)
    while events:
        t, _, kind, (d, *rest) = heapq.heappop(events)
        z, y = d
        if kind == "queue":
            k, part, there = rest
            u = z if y == 0 else length - 1 - z
            c = mirrored_part(length, y, part)
            if c < 8 * length:
                order = c % 4 // 2 - abs(c // 8 - u) * (0.5 if k == ACROSS else 1.0)
            else:
                order = rank[c // 4 * 4]
            heapq.heappush(queues.setdefault((d, k), []), ((order, c), there, part))
            if not busy.get((d, k)):
                busy[d, k] = True
                push(t, "launch", d, k)
        elif kind == "launch":
            launch(t, d, rest[0])
        elif kind == "sent":
            k, there = rest
            push(t + 1.75, "landed", ((z - 1, y), (z + 1, y), (z, 1 - y))[k], there)
            launch(t, d, k)
        else:
            landed[d][rest[0]] = t
            offer(t + 0.3, d, rest[0])
            if z in (1, length - 2) and d not in answered:
                far = [
                    (2 * sz + sy) * 4 + sp
                    for sz, sy, sp in itertools.product(range(length), range(2), range(2))
                    if not needs(length, 0 if z == 1 else length - 1, sz, 0) and sz != z
                ]
                if all(p in landed[d] for p in (q_far, q_far + 1, *far)):
                    answered.add(d)
                    for k in range(2):
                        offer(t + 2.5, d, o_own + k)
    programs = []
    for z in range(length):
        d = (z, 0)
        timed = [(t, 1, p) for p, t in landed[d].items()]
        timed += [(-2.0, 0, 8 * z + k) for k in range(2)]
        if z in ends:
            timed += [(-1.0, 0, q_own + k) for k in range(2)]
        for p in (8 * z + 2, 8 * z + 3, *range(own_edge, own_edge + 4)):
            timed.append((max(0.0, left[d, p] - 1.0), 0, p))
        timed.sort()
        codes = [p * 16 + 8 * waits + sum(2**k for k, _ in sends[d].get(p, [])) for _, waits, p in timed]
        in_loop = 1 + max(i for i, (_, _, p) in enumerate(timed) if p < 8 * length)
        results = [i + 1 for i, (_, _, p) in enumerate(timed) if p >= o_far]
        complete, queries = {}, 0
        for i, (_, _, p) in enumerate(timed):
            if p < 8 * length and needs(length, z, p // 8, p % 4 // 2):
                complete[p % 4 // 2, p // 8] = i + 1
            if q_far <= p < q_far + 2:
                queries = i + 1
        steps, bounds, top, helped = [], [], 0, False
        chosen = sorted(complete, key=lambda k: (k[0], complete[k]))
        for i, (sample, sz) in enumerate(chosen):
            top = max(top, complete[sample, sz])
            flags = 0
            if z in (1, length - 2) and sample == 0:
                if not needs(length, 0 if z == 1 else length - 1, sz, 0):
                    flags, helped, top = 1 if helped else 3, True, max(top, queries)
                if i == length - 1:
                    flags += 4
            steps.append((sample, sz, flags))
            bounds.append(top)
        programs.append((codes, in_loop, max([in_loop, *results]), steps, bounds))
    return programs


def device_plan(length):
    n = 2 * length
    programs = TUNED.get(length) or programs_by_time(length)
    plan = {name: [] for name in ("ops", "bounds", "steps", "n_steps", "in_loop", "to_merge", "n_ops")}
    plan["sent"] = [[0] * n for _ in range(3)]
    for d in range(n):
        z, y = divmod(d, 2)
        codes, in_loop, to_merge, steps, bounds = programs[z if y == 0 else length - 1 - z]
        ops = []
        for code in codes:
            where = code % 8
            if y == 1:
                where = where // 4 * 4 + where // 2 % 2 + where % 2 * 2
            ops.append(mirrored_part(length, y, code // 16) * 16 + code // 8 % 2 * 8 + where)
            for k in range(3):
                plan["sent"][k][d] += where // 2**k % 2
        plan["ops"].append(ops)
        plan["bounds"].append([*bounds, in_loop])
        plan["steps"].append(
            [s + 2 * (sz if y == 0 else length - 1 - sz) + 512 * flags for s, sz, flags in steps]
        )
        for name, value in zip(("n_steps", "in_loop", "to_merge", "n_ops"), (len(steps), in_loop, to_merge, len(ops))):
            plan[name].append(value)
    for name in ("ops", "bounds", "steps"):
        width = max(len(row) for row in plan[name])
        plan[name] = [row + [0] * (width - len(row)) for row in plan[name]]
    return plan


def layer_norm(values, gain, bias):
    values = values.astype(F32)
    centre = jnp.mean(values, -1, keepdims=True)
    centred = values - centre
    spread = jnp.mean(centred * centred, -1, keepdims=True)
    return (centred * lax.rsqrt(spread + EPSILON) * gain + bias).astype(BF16)


def dot(a, b):
    return jnp.dot(a, b, preferred_element_type=F32)


def split_dot(a, b):
    high = a.astype(BF16)
    rest = a - high.astype(F32)
    mid = rest.astype(BF16)
    low = (rest - mid.astype(F32)).astype(BF16)
    return dot(high, b) + dot(mid, b) + dot(low, b)


def kernel(
    n,
    plan,
    hidden_hbm,
    stale_attn_hbm,
    stale_conv_hbm,
    ln_gain_hbm,
    ln_bias_hbm,
    w_qkv_hbm,
    w_out_hbm,
    gn_gain_hbm,
    gn_bias_hbm,
    conv_w_hbm,
    conv_bias_hbm,
    time_shift_hbm,
    out,
    hidden,
    stale_attn,
    ln_gain,
    ln_bias,
    gn_gain,
    gn_bias,
    conv_bias,
    time_shift,
    w_qkv,
    w_out,
    conv_w,
    blocks,
    keys,
    values,
    q_diag,
    soft,
    soft_far,
    accum,
    same_group,
    conv_acc,
    stats,
    load_sem,
    vector_sem,
    send_sem,
    recv_sem,
    soft_sem,
    stat_sem,
):
    samples, _, cols, channels = out.shape
    tokens = samples * cols
    pairs = channels // (2 * HEAD_DIM)
    group_size = channels // GROUPS
    length = n // 2
    own_edge, cross, handed, q_own, q_far, o_own, o_far = special_parts(length)
    fresh_part = 4 * n
    me = lax.axis_index("patch")
    z = me // 2
    y = me % 2
    above_exists = z > 0
    below_exists = z < length - 1
    neighbours = ((above_exists, me - 2), (below_exists, me + 2), (True, z * 2 + 1 - y))

    barrier = pltpu.get_barrier_semaphore()
    for there, device in neighbours:
        def announce(device=device):
            pl.semaphore_signal(barrier, inc=1, device_id={"patch": device}, device_id_type=MESH)
        if there is True:
            announce()
        else:
            pl.when(there)(announce)

    load_stale = pltpu.make_async_copy(stale_attn_hbm, stale_attn, load_sem.at[0])
    load_hidden = pltpu.make_async_copy(hidden_hbm, hidden, load_sem.at[1])
    load_qkv = pltpu.make_async_copy(w_qkv_hbm, w_qkv, load_sem.at[2])
    load_edge = pltpu.make_async_copy(stale_conv_hbm, blocks.at[pl.ds(own_edge, 4)], load_sem.at[3])
    load_out = pltpu.make_async_copy(w_out_hbm, w_out, load_sem.at[4])
    load_conv = pltpu.make_async_copy(conv_w_hbm, conv_w, load_sem.at[5])
    load_shift = pltpu.make_async_copy(time_shift_hbm, time_shift, load_sem.at[6])
    vectors = [
        pltpu.make_async_copy(source, target, vector_sem.at[i])
        for i, (source, target) in enumerate(
            (
                (ln_gain_hbm, ln_gain),
                (ln_bias_hbm, ln_bias),
                (gn_gain_hbm, gn_gain),
                (gn_bias_hbm, gn_bias),
                (conv_bias_hbm, conv_bias),
            )
        )
    ]
    load_stale.start()
    for load in vectors[:2]:
        load.start()
    load_hidden.start()
    load_qkv.start()
    load_edge.start()
    for load in vectors[2:]:
        load.start()
    load_shift.start()
    load_out.start()
    load_conv.start()

    def pick(choices):
        if len(set(choices)) == 1:
            return jnp.int32(choices[0])
        value = jnp.int32(choices[0])
        for k in range(1, n):
            value = jnp.where(me == k, jnp.int32(choices[k]), value)
        return value

    def table(name):
        rows = plan[name]
        bits = max(v for row in rows for v in row).bit_length()
        per = 31 // bits
        words = [
            pick([sum(v << (bits * k) for k, v in enumerate(row[at : at + per])) for row in rows])
            for at in range(0, len(rows[0]), per)
        ]

        def look(i):
            word = words[0]
            for k in range(1, len(words)):
                word = jnp.where(i // per == k, words[k], word)
            return lax.shift_right_logical(word, i % per * bits) & (2**bits - 1)

        return look

    ops, bounds, steps = table("ops"), table("bounds"), table("steps")
    n_steps = pick(plan["n_steps"])
    in_loop = pick(plan["in_loop"])
    to_merge = pick(plan["to_merge"])
    n_ops = pick(plan["n_ops"])
    soft[...] = jnp.zeros_like(soft)
    for slot in range(samples + 1):
        soft[slot, 0] = jnp.full(soft.shape[2:], -jnp.inf, F32)
    accum[...] = jnp.zeros_like(accum)
    q_diag[...] = jnp.zeros_like(q_diag)

    @pl.when(jnp.where(y == 0, z == 0, z == length - 1))
    def _():
        blocks[handed : handed + 4] = jnp.zeros_like(blocks[handed : handed + 4])

    mine = me * 4
    per_sample = 2
    for load in vectors[:2]:
        load.wait()
    load_stale.wait()

    def pump(i, carry):
        op = ops(i)
        part = op // 16
        landed = jnp.where(part < 4 * n, part, part - 8)

        @pl.when(op // 8 % 2 == 1)
        def _():
            pltpu.make_async_remote_copy(
                src_ref=blocks.at[part],
                dst_ref=blocks.at[part],
                send_sem=send_sem.at[0],
                recv_sem=recv_sem.at[landed],
                device_id={"patch": z * 2 + 1 - y},
                device_id_type=MESH,
            ).wait_recv()

        there = jnp.where(part < 4 * n, part, part + 4)
        landing = jnp.where(part < 4 * n, part, part - 4)
        for k, (_, device) in enumerate(neighbours):

            @pl.when(op // 2**k % 2 == 1)
            def _(k=k, device=device):
                pltpu.make_async_remote_copy(
                    src_ref=blocks.at[part],
                    dst_ref=blocks.at[there],
                    send_sem=send_sem.at[k],
                    recv_sem=recv_sem.at[landing],
                    device_id={"patch": device},
                    device_id_type=MESH,
                ).start()

        return carry

    def pumps(first, last):
        lax.fori_loop(first, last, pump, 0)

    def norm_stale(s):
        part = layer_norm(stale_attn[2 * s : 2 * s + 2], ln_gain[...], ln_bias[...])
        blocks[pl.ds(mine + 2 * s, 2)] = part

    norm_stale(0)
    pl.semaphore_wait(barrier, 1 + above_exists.astype(jnp.int32) + below_exists.astype(jnp.int32))
    pumps(0, 2)
    for s in range(1, samples):
        norm_stale(s)

    load_hidden.wait()
    fresh = layer_norm(hidden[...], ln_gain[...], ln_bias[...])
    blocks[fresh_part : fresh_part + 4] = fresh.reshape(4, tokens // 4, channels)
    load_qkv.wait()
    queries = dot(fresh, w_qkv[:, :channels]).astype(BF16).astype(F32) * HEAD_DIM ** (-0.5)
    if MOVED:
        blocks[q_own : q_own + 2] = queries[:cols].astype(BF16).reshape(2, cols // 2, channels)

    def spread_queries(slot, q_t):
        for pair in range(pairs):
            for half in range(2):
                row = (2 * pair + half) * HEAD_DIM
                q_diag[
                    slot, pair, half * HEAD_DIM : (half + 1) * HEAD_DIM, half * cols : (half + 1) * cols
                ] = q_t[row : row + HEAD_DIM]

    q_t = queries.T.astype(BF16)
    for s in range(samples):
        spread_queries(s, q_t[:, s * cols : (s + 1) * cols])
    load_edge.wait()
    pumps(2, bounds(0))
    channel_row = lax.broadcasted_iota(jnp.int32, (channels, channels), 0) // group_size
    channel_col = lax.broadcasted_iota(jnp.int32, (channels, channels), 1) // group_size
    same_group[...] = jnp.where(channel_row == channel_col, 1.0, 0.0).astype(BF16)

    def attend(slot):
        lanes = [slice(pair * 2 * HEAD_DIM, (pair + 1) * 2 * HEAD_DIM) for pair in range(pairs)]
        old_max, old_sum = soft[slot, 0], soft[slot, 1]
        scores = [dot(keys[:, lanes[pair]], q_diag[slot, pair]) for pair in range(pairs)]
        new_max = [
            jnp.maximum(old_max[pair : pair + 1], jnp.max(scores[pair], 0, keepdims=True))
            for pair in range(pairs)
        ]
        weights = [jnp.exp(scores[pair] - new_max[pair]) for pair in range(pairs)]
        both = [lax.dot_general(
                values[:, lanes[pair]],
                weights[pair].astype(BF16),
                (((0,), (0,)), ((), ())),
                preferred_element_type=F32,
            )
            for pair in range(pairs)]
        rescale = [jnp.exp(old_max[pair : pair + 1] - new_max[pair]) for pair in range(pairs)]
        soft[slot, 0] = jnp.concatenate(new_max, 0)
        soft[slot, 1] = jnp.concatenate(
            [
                jnp.sum(weights[pair], 0, keepdims=True) + old_sum[pair : pair + 1] * rescale[pair]
                for pair in range(pairs)
            ],
            0,
        )
        for pair in range(pairs):
            for half in range(2):
                row = (2 * pair + half) * HEAD_DIM
                own = slice(half * cols, (half + 1) * cols)
                accum[slot, row : row + HEAD_DIM] = (
                    both[pair][half * HEAD_DIM : (half + 1) * HEAD_DIM, own]
                    + accum[slot, row : row + HEAD_DIM] * rescale[pair][:, own]
                )

    def normalised(slot):
        for head in range(2 * pairs):
            row = head * HEAD_DIM
            total = soft[slot, 1, head // 2 : head // 2 + 1, (head % 2) * cols : (head % 2 + 1) * cols]
            accum[slot, row : row + HEAD_DIM] = accum[slot, row : row + HEAD_DIM] / total
        return accum[slot].T

    def soft_copy(device):
        return pltpu.make_async_remote_copy(
            src_ref=soft.at[samples],
            dst_ref=soft_far,
            send_sem=soft_sem.at[0],
            recv_sem=soft_sem.at[1],
            device_id={"patch": device},
            device_id_type=MESH,
        )

    at_end = (z == 0) | (z == length - 1)
    helps = (z == 1) | (z == length - 2)
    outward = jnp.where(z == 1, me - 2, me + 2)

    def step(i, carry):
        code = steps(i)
        s = code % 2
        sz = code // 2 % 256
        first_slot = jnp.where(sz == z, n, 2 * sz + y)
        second_slot = 2 * sz + 1 - y
        low = bounds(i)
        span = bounds(i + 1) - low
        marks = [low + span * k // 2 for k in range(3)]
        rows = jnp.concatenate(
            [
                blocks[pl.ds(slot * 4 + 2 * s, 2)].reshape(cols, channels)
                for slot in (first_slot, second_slot)
            ],
            0,
        )
        both_kv = dot(rows, w_qkv[:, channels:]).astype(BF16)
        keys[...] = both_kv[:, :channels]
        values[...] = both_kv[:, channels:]
        pumps(marks[0], marks[1])
        attend(s)
        pumps(marks[1], marks[2])
        if MOVED:
            flag = code // 512

            @pl.when(flag % 2 == 1)
            def _():
                @pl.when(flag // 2 % 2 == 1)
                def _():
                    far = blocks[q_far : q_far + 2].reshape(cols, channels)
                    spread_queries(samples, far.astype(F32).T.astype(BF16))

                attend(samples)

            @pl.when(flag // 4 % 2 == 1)
            def _():
                part = normalised(samples).astype(BF16)
                blocks[o_own : o_own + 2] = part.reshape(2, cols // 2, channels)
                soft_copy(outward).start()
                for k in range(2):
                    pltpu.make_async_remote_copy(
                        src_ref=blocks.at[o_own + k],
                        dst_ref=blocks.at[o_far + k],
                        send_sem=soft_sem.at[2 + k],
                        recv_sem=recv_sem.at[o_far + k - 8],
                        device_id={"patch": outward},
                        device_id_type=MESH,
                    ).start()

        return carry

    lax.fori_loop(0, n_steps, step, 0)
    if MOVED:
        pumps(in_loop, to_merge)

        @pl.when(at_end)
        def _():
            soft_copy(z * 2 + 1 - y).wait_recv()
            far = blocks[o_far : o_far + 2].reshape(cols, channels).astype(F32).T
            for head in range(2 * pairs):
                row = head * HEAD_DIM
                at = (slice(head // 2, head // 2 + 1), slice((head % 2) * cols, (head % 2 + 1) * cols))
                near_max, far_max = soft[(0, 0, *at)], soft_far[(0, *at)]
                top = jnp.maximum(near_max, far_max)
                near_scale = jnp.exp(near_max - top)
                far_sum = soft_far[(1, *at)] * jnp.exp(far_max - top)
                accum[0, row : row + HEAD_DIM] = (
                    accum[0, row : row + HEAD_DIM] * near_scale + far[row : row + HEAD_DIM] * far_sum
                )
                soft[(0, 1, *at)] = soft[(0, 1, *at)] * near_scale + far_sum

    attended = jnp.concatenate([normalised(s) for s in range(samples)], 0).astype(BF16)
    load_out.wait()
    residual = hidden[...].astype(F32) + dot(attended, w_out[...])
    residual = residual.astype(BF16).astype(F32).reshape(samples, cols, channels)

    sum_rows = jnp.concatenate([jnp.sum(residual[s], 0, keepdims=True) for s in range(samples)], 0)
    cells = cols * group_size
    local_mean = split_dot(sum_rows, same_group[...]) / cells
    centred = residual - local_mean[:, None, :]
    square_rows = jnp.concatenate(
        [jnp.sum(centred[s] * centred[s], 0, keepdims=True) for s in range(samples)], 0
    )
    local_square = split_dot(square_rows, same_group[...])
    stats[me, :samples] = local_mean
    stats[me, samples:] = local_square

    def stat_copy(distance):
        return pltpu.make_async_remote_copy(
            src_ref=stats.at[me],
            dst_ref=stats.at[me],
            send_sem=stat_sem.at[0],
            recv_sem=stat_sem.at[1],
            device_id={"patch": lax.rem(me + distance, n)},
            device_id_type=MESH,
        )

    for distance in range(1, n):
        stat_copy(distance).start()

    pumps(to_merge, n_ops)
    load_conv.wait()
    above = blocks[pl.ds(jnp.where(y == 0, handed, cross), 4)].reshape(tokens, channels)
    below = blocks[pl.ds(jnp.where(y == 0, cross, handed), 4)].reshape(tokens, channels)
    for tap in range(3):
        conv_acc[tap] = dot(above, conv_w[0, tap]) + dot(below, conv_w[2, tap])
    for load in vectors[2:]:
        load.wait()
    load_shift.wait()

    others = stats.at[pl.ds(0, n - 1)]
    pltpu.make_async_remote_copy(
        src_ref=others,
        dst_ref=others,
        send_sem=stat_sem.at[0],
        recv_sem=stat_sem.at[1],
        device_id={"patch": z * 2 + 1 - y},
        device_id_type=MESH,
    ).wait_recv()
    every = stats[...]
    group_mean = jnp.mean(every[:, :samples], 0)
    shift = every[:, :samples] - group_mean[None]
    group_var = (jnp.sum(every[:, samples:], 0) + cells * jnp.sum(shift * shift, 0)) / (cells * n)
    scale = lax.rsqrt(group_var + EPSILON)
    pre = (residual - group_mean[:, None, :]) * scale[:, None, :] * gn_gain[...] + gn_bias[...]
    activated = (pre / (1.0 + jnp.exp(-pre))).astype(BF16).reshape(tokens, channels)

    column = lax.broadcasted_iota(jnp.int32, (tokens, 1), 0) % cols
    total = conv_acc[1] + dot(activated, conv_w[1, 1])
    left = pltpu.roll(conv_acc[0] + dot(activated, conv_w[1, 0]), 1, 0)
    total = total + jnp.where(column == 0, 0.0, left)
    right = pltpu.roll(conv_acc[2] + dot(activated, conv_w[1, 2]), tokens - 1, 0)
    total = total + jnp.where(column == cols - 1, 0.0, right)
    total = total.reshape(samples, cols, channels) + conv_bias[...]
    for sample in range(samples):
        out[sample, 0] = (
            total[sample] + time_shift[sample : sample + 1] + residual[sample]
        ).astype(BF16)

    def sent(source, semaphore):
        pltpu.make_async_remote_copy(
            src_ref=source,
            dst_ref=source,
            send_sem=semaphore,
            recv_sem=stat_sem.at[1],
            device_id={"patch": z * 2 + 1 - y},
            device_id_type=MESH,
        ).wait_send()

    sent(others, stat_sem.at[0])
    for k in range(3):
        for count in sorted(set(plan["sent"][k]) - {0}):
            those = [d for d in range(n) if plan["sent"][k][d] == count]
            match = functools.reduce(jnp.logical_or, [me == d for d in those])
            pl.when(match)(lambda: sent(blocks.at[pl.ds(0, count)], send_sem.at[k]))
    if MOVED:

        @pl.when(helps)
        def _():
            sent(soft.at[samples], soft_sem.at[0])
            for k in range(2):
                sent(blocks.at[o_own + k], soft_sem.at[2 + k])


def shards(n, *arrays):
    (hidden, stale_attn, stale_conv, ln_gain, ln_bias, w_qkv, w_out) = arrays[:7]
    (gn_gain, gn_bias, conv_w, conv_bias, time_shift) = arrays[7:]
    samples, rows_dev, cols, channels = hidden.shape
    assert rows_dev == 1 and samples == 2 and n % 2 == 0 and n >= 8, "unsupported split"
    tokens = samples * cols
    pairs = channels // (2 * HEAD_DIM)
    hbm = pl.BlockSpec(memory_space=pl.ANY)
    vmem = pl.BlockSpec(memory_space=pltpu.VMEM)
    dma = pltpu.SemaphoreType.DMA
    plan = device_plan(n // 2)
    parts = 4 * (n + 8)
    slots = samples + 1 if MOVED else samples
    return pl.pallas_call(
        functools.partial(kernel, n, plan),
        out_shape=pltpu.VMEM(hidden.shape, BF16),
        in_specs=[hbm] * 12,
        out_specs=vmem,
        scratch_shapes=[
            pltpu.VMEM((tokens, channels), BF16),
            pltpu.VMEM((4, tokens // 4, channels), BF16),
        ]
        + [pltpu.VMEM((channels,), F32)] * 5
        + [
            pltpu.VMEM(time_shift.shape, F32),
            pltpu.VMEM(w_qkv.shape, BF16),
            pltpu.VMEM(w_out.shape, BF16),
            pltpu.VMEM(conv_w.shape, BF16),
            pltpu.VMEM((parts, tokens // 4, channels), BF16),
            pltpu.VMEM((2 * cols, channels), BF16),
            pltpu.VMEM((2 * cols, channels), BF16),
            pltpu.VMEM((samples + 1, pairs, 2 * HEAD_DIM, 2 * cols), BF16),
            pltpu.VMEM((samples + 1, 2, pairs, 2 * cols), F32),
            pltpu.VMEM((2, pairs, 2 * cols), F32),
            pltpu.VMEM((samples + 1, channels, cols), F32),
            pltpu.VMEM((channels, channels), BF16),
            pltpu.VMEM((3, tokens, channels), F32),
            pltpu.VMEM((n, 2 * samples, channels), F32),
            dma((7,)),
            dma((5,)),
            dma((3,)),
            dma((4 * n + (22 if MOVED else 8),)),
            dma((4,)),
            dma((2,)),
        ],
        compiler_params=pltpu.CompilerParams(
            collective_id=0, has_side_effects=True, vmem_limit_bytes=56 * 2**20
        ),
        name="section",
    )(
        hidden.reshape(tokens, channels),
        stale_attn.reshape(4, tokens // 4, channels),
        stale_conv.reshape(4, tokens // 4, channels),
        ln_gain,
        ln_bias,
        w_qkv,
        w_out,
        gn_gain,
        gn_bias,
        conv_w,
        conv_bias,
        time_shift,
    )


def solution(mesh):
    wide = P("img", "patch", None, None)
    in_specs = (wide, wide, wide) + (P(),) * 8 + (P("img", None),)
    body = functools.partial(shards, mesh.shape["patch"])
    return jax.shard_map(body, mesh=mesh, in_specs=in_specs, out_specs=wide, check_vma=False)
```

time: 56 us -> 44.7 us (0.80)
  Pallas kernels: 54.1 us -> 43.8 us
  local copies, waits for them, and re-layouts: 1.73 us -> 0.73 us
    pallas_call x1, Pallas kernels: 54.1 us -> 43.8 us  [shards(): pl.pallas_call(functools.partial(kernel, n, plan), out_shape=pltpu.VMEM(h...]
    unnamed x1, local copies, waits for them, and re-layouts: 1.73 us -> 0.73 us
where the time goes in v1:
time: 44.7 us; the launch traced here: 44.6 us
  Pallas kernels  43.8 us (98%)
  local copies, waits for them, and re-layouts  0.73 us (2%)
    pallas_call x1, Pallas kernels, shards(): pl.pallas_call(functools.partial(kernel, n, plan), out_shape=pltpu.VMEM(h...  43.8 us

profile of v1, /device:TPU:0, one launch (start us, length us, event | category | flops | bytes accessed | tf_op | source)
XLA Modules:
  0.0 44.6 jit_solution(12721705543658793931)
XLA Ops:
  0.0 43.8 %section.1 = bf16[2,1,128,640]{3,2,1,0:T(8,128)(2,1)S(1)} custom-call(bf16[256,640]{1,0:T(8,128)(2,1)} %bitcast.3, bf16[4,64,640]{2,1,0:T(8,128)(2,1)} %bitcast.4, bf16[4,64,640]{2,1,0:T(8,128)(2,1)} %bitcast.5, f32[640]{0:T(1024)} %ln_gain_hbm.1, f32[640]{0:T(1024)} %ln_bias_hbm.1, bf16[640,1920]{1,0:T(8,128)(2,1)} %w_qkv_hbm.1, ...), custom_call_target="tpu_custom_call" | custom-call | tf_op jit(solution)/shard_map/section/pallas_call | solution.py:694
  43.8 0.7 %copy.14 = bf16[2,1,128,640]{3,2,1,0:T(8,128)(2,1)} copy(bf16[2,1,128,640]{3,2,1,0:T(8,128)(2,1)S(1)} %section.1) | data formatting | bytes 655360

commit v2 on v1

--- a/solution.py
+++ b/solution.py
@@ -21,32 +21,32 @@
 TUNED = {
     4: [
         (
-            [6, 22, 770, 786, 612, 38, 88, 140, 122, 152, 54, 580, 74, 188, 248, 316, 200, 216, 300, 682, 628, 232, 666, 596, 106, 168, 360, 376, 444, 698, 428, 650, 488, 984, 504, 968],
+            [6, 22, 54, 38, 612, 770, 786, 136, 90, 628, 122, 74, 172, 152, 650, 188, 248, 316, 106, 300, 698, 232, 428, 200, 444, 376, 360, 580, 596, 216, 488, 504, 968, 682, 984, 666],
+            32,
             35,
-            36,
-            [(0, 0, 0), (0, 1, 0), (1, 0, 0), (1, 1, 0), (1, 2, 0), (1, 3, 0)],
-            [13, 18, 25, 26, 28, 35],
+            [(0, 0, 0), (1, 0, 0), (1, 1, 0), (1, 2, 0), (0, 1, 0), (1, 3, 0)],
+            [12, 19, 22, 27, 30, 32],
         ),
         (
-            [135, 151, 167, 596, 183, 580, 10, 219, 313, 30, 200, 280, 235, 297, 840, 42, 268, 328, 88, 120, 412, 58, 360, 650, 628, 72, 396, 456, 445, 472, 856, 250, 429, 744, 344, 698, 728, 612, 104, 488, 376, 666, 682, 760, 504, 712],
-            45,
-            45,
-            [(0, 1, 0), (0, 0, 0), (0, 3, 3), (0, 2, 5), (1, 1, 0), (1, 0, 0), (1, 2, 0), (1, 3, 0)],
-            [11, 26, 31, 35, 35, 39, 41, 45],
+            [135, 151, 167, 10, 268, 284, 26, 201, 183, 42, 313, 396, 58, 217, 328, 234, 250, 840, 412, 297, 580, 856, 628, 429, 344, 596, 88, 445, 472, 456, 72, 120, 360, 104, 666, 612, 376, 650, 712, 488, 682, 504, 698, 760, 744, 728],
+            42,
+            42,
+            [(0, 1, 0), (1, 1, 0), (0, 2, 3), (0, 3, 5), (0, 0, 0), (1, 0, 0), (1, 2, 0), (1, 3, 0)],
+            [14, 17, 25, 30, 31, 34, 37, 42],
         ),
         (
-            [263, 279, 311, 295, 140, 363, 393, 170, 413, 666, 580, 186, 328, 425, 12, 456, 650, 28, 441, 472, 216, 347, 488, 628, 152, 200, 840, 46, 88, 856, 596, 232, 377, 612, 62, 698, 72, 712, 104, 248, 120, 760, 682, 504, 728, 744],
-            44,
-            44,
-            [(0, 3, 0), (0, 2, 0), (0, 1, 3), (0, 0, 5), (1, 2, 0), (1, 1, 0), (1, 0, 0), (1, 3, 0)],
-            [20, 22, 30, 37, 37, 40, 41, 44],
+            [263, 279, 311, 140, 393, 409, 346, 330, 295, 156, 12, 425, 170, 216, 28, 441, 580, 186, 596, 377, 361, 840, 612, 46, 200, 856, 504, 72, 62, 88, 650, 488, 456, 628, 248, 232, 104, 472, 666, 698, 120, 682, 712, 728, 744, 760],
+            41,
+            41,
+            [(0, 2, 0), (1, 2, 0), (0, 1, 3), (0, 0, 5), (1, 3, 0), (1, 1, 0), (0, 3, 0), (1, 0, 0)],
+            [8, 21, 26, 30, 32, 36, 38, 41],
         ),
         (
-            [389, 405, 769, 785, 437, 421, 316, 457, 268, 680, 612, 296, 489, 596, 328, 360, 472, 728, 172, 648, 188, 248, 628, 376, 712, 580, 232, 344, 280, 696, 44, 664, 505, 60, 120, 760, 104, 968, 984, 744],
-            37,
-            39,
-            [(0, 3, 0), (0, 2, 0), (1, 2, 0), (1, 1, 0), (1, 3, 0), (1, 0, 0)],
-            [17, 29, 29, 29, 33, 37],
+            [389, 405, 580, 437, 785, 280, 421, 769, 628, 505, 344, 316, 300, 172, 489, 457, 360, 188, 376, 44, 696, 473, 60, 612, 264, 232, 248, 596, 328, 104, 968, 120, 712, 984, 664, 760, 648, 728, 680, 744],
+            32,
+            34,
+            [(1, 3, 0), (1, 2, 0), (0, 3, 0), (1, 1, 0), (0, 2, 0), (1, 0, 0)],
+            [15, 19, 22, 27, 29, 32],
         ),
     ]
 }
@@ -180,25 +180,27 @@
             if q_far <= p < q_far + 2:
                 queries = i + 1
         steps, bounds, top, helped = [], [], 0, False
-        chosen = sorted(complete, key=lambda k: (k[0], complete[k]))
+        chosen = sorted(complete, key=lambda k: (complete[k], k))
         for i, (sample, sz) in enumerate(chosen):
             top = max(top, complete[sample, sz])
             flags = 0
             if z in (1, length - 2) and sample == 0:
                 if not needs(length, 0 if z == 1 else length - 1, sz, 0):
                     flags, helped, top = 1 if helped else 3, True, max(top, queries)
-                if i == length - 1:
-                    flags += 4
-            steps.append((sample, sz, flags))
+                    last_far = i
+            steps.append([sample, sz, flags])
             bounds.append(top)
+        if z in (1, length - 2):
+            steps[last_far][2] += 4
         programs.append((codes, in_loop, max([in_loop, *results]), steps, bounds))
     return programs
 
 
 def device_plan(length):
     n = 2 * length
+    cross = special_parts(length)[1]
     programs = TUNED.get(length) or programs_by_time(length)
-    plan = {name: [] for name in ("ops", "bounds", "steps", "n_steps", "in_loop", "to_merge", "n_ops")}
+    plan = {name: [] for name in ("ops", "bounds", "steps", "n_steps", "in_loop", "to_merge", "crossed", "n_ops")}
     plan["sent"] = [[0] * n for _ in range(3)]
     for d in range(n):
         z, y = divmod(d, 2)
@@ -216,8 +218,12 @@
         plan["steps"].append(
             [s + 2 * (sz if y == 0 else length - 1 - sz) + 512 * flags for s, sz, flags in steps]
         )
-        for name, value in zip(("n_steps", "in_loop", "to_merge", "n_ops"), (len(steps), in_loop, to_merge, len(ops))):
-            plan[name].append(value)
+        across = [i + 1 for i, code in enumerate(codes) if cross <= code // 16 < cross + 4]
+        plan["n_steps"].append(len(steps))
+        plan["in_loop"].append(in_loop)
+        plan["to_merge"].append(to_merge)
+        plan["crossed"].append(max(to_merge, *across))
+        plan["n_ops"].append(len(ops))
     for name in ("ops", "bounds", "steps"):
         width = max(len(row) for row in plan[name])
         plan[name] = [row + [0] * (width - len(row)) for row in plan[name]]
@@ -236,12 +242,22 @@
     return jnp.dot(a, b, preferred_element_type=F32)
 
 
+def balanced_dot(a, b):
+    wide = b.shape[1] // 512 * 512
+    half = a.shape[0] // 2
+    rest = b[:, wide:]
+    tail = jnp.concatenate([dot(a[:half], rest), dot(a[half:], rest)], 0)
+    return jnp.concatenate([dot(a, b[:, :wide]), tail], 1)
+
+
 def split_dot(a, b):
     high = a.astype(BF16)
     rest = a - high.astype(F32)
     mid = rest.astype(BF16)
     low = (rest - mid.astype(F32)).astype(BF16)
-    return dot(high, b) + dot(mid, b) + dot(low, b)
+    rows = a.shape[0]
+    thirds = dot(jnp.concatenate([high, mid, low], 0), b)
+    return thirds[:rows] + thirds[rows : 2 * rows] + thirds[2 * rows :]
 
 
 def kernel(
@@ -316,7 +332,15 @@
     load_qkv = pltpu.make_async_copy(w_qkv_hbm, w_qkv, load_sem.at[2])
     load_edge = pltpu.make_async_copy(stale_conv_hbm, blocks.at[pl.ds(own_edge, 4)], load_sem.at[3])
     load_out = pltpu.make_async_copy(w_out_hbm, w_out, load_sem.at[4])
-    load_conv = pltpu.make_async_copy(conv_w_hbm, conv_w, load_sem.at[5])
+    load_conv = [
+        pltpu.make_async_copy(
+            conv_w_hbm.at[row, tap],
+            conv_w.at[row, :, pl.ds(tap * channels, channels)],
+            load_sem.at[5],
+        )
+        for row in range(3)
+        for tap in range(3)
+    ]
     load_shift = pltpu.make_async_copy(time_shift_hbm, time_shift, load_sem.at[6])
     vectors = [
         pltpu.make_async_copy(source, target, vector_sem.at[i])
@@ -334,13 +358,6 @@
     for load in vectors[:2]:
         load.start()
     load_hidden.start()
-    load_qkv.start()
-    load_edge.start()
-    for load in vectors[2:]:
-        load.start()
-    load_shift.start()
-    load_out.start()
-    load_conv.start()
 
     def pick(choices):
         if len(set(choices)) == 1:
@@ -371,6 +388,7 @@
     n_steps = pick(plan["n_steps"])
     in_loop = pick(plan["in_loop"])
     to_merge = pick(plan["to_merge"])
+    crossed = pick(plan["crossed"])
     n_ops = pick(plan["n_ops"])
     soft[...] = jnp.zeros_like(soft)
     for slot in range(samples + 1):
@@ -387,6 +405,14 @@
     for load in vectors[:2]:
         load.wait()
     load_stale.wait()
+    load_qkv.start()
+    load_edge.start()
+    for load in vectors[2:]:
+        load.start()
+    load_shift.start()
+    load_out.start()
+    for load in load_conv:
+        load.start()
 
     def pump(i, carry):
         op = ops(i)
@@ -497,7 +523,7 @@
         for head in range(2 * pairs):
             row = head * HEAD_DIM
             total = soft[slot, 1, head // 2 : head // 2 + 1, (head % 2) * cols : (head % 2 + 1) * cols]
-            accum[slot, row : row + HEAD_DIM] = accum[slot, row : row + HEAD_DIM] / total
+            accum[slot, row : row + HEAD_DIM] = accum[slot, row : row + HEAD_DIM] * (1.0 / total)
         return accum[slot].T
 
     def soft_copy(device):
@@ -530,7 +556,7 @@
             ],
             0,
         )
-        both_kv = dot(rows, w_qkv[:, channels:]).astype(BF16)
+        both_kv = balanced_dot(rows, w_qkv[:, channels:]).astype(BF16)
         keys[...] = both_kv[:, :channels]
         values[...] = both_kv[:, channels:]
         pumps(marks[0], marks[1])
@@ -587,7 +613,7 @@
 
     attended = jnp.concatenate([normalised(s) for s in range(samples)], 0).astype(BF16)
     load_out.wait()
-    residual = hidden[...].astype(F32) + dot(attended, w_out[...])
+    residual = hidden[...].astype(F32) + balanced_dot(attended, w_out[...])
     residual = residual.astype(BF16).astype(F32).reshape(samples, cols, channels)
 
     sum_rows = jnp.concatenate([jnp.sum(residual[s], 0, keepdims=True) for s in range(samples)], 0)
@@ -614,12 +640,12 @@
     for distance in range(1, n):
         stat_copy(distance).start()
 
-    pumps(to_merge, n_ops)
-    load_conv.wait()
-    above = blocks[pl.ds(jnp.where(y == 0, handed, cross), 4)].reshape(tokens, channels)
-    below = blocks[pl.ds(jnp.where(y == 0, cross, handed), 4)].reshape(tokens, channels)
-    for tap in range(3):
-        conv_acc[tap] = dot(above, conv_w[0, tap]) + dot(below, conv_w[2, tap])
+    pumps(to_merge, crossed)
+    pltpu.make_async_copy(conv_w, conv_w, load_sem.at[5]).wait()
+    cross_row = jnp.where(y == 0, 2, 0)
+    conv_acc[...] = dot(blocks[cross : cross + 4].reshape(tokens, channels), conv_w[cross_row])
+    pumps(crossed, n_ops)
+    conv_acc[...] += dot(blocks[handed : handed + 4].reshape(tokens, channels), conv_w[2 - cross_row])
     for load in vectors[2:]:
         load.wait()
     load_shift.wait()
@@ -642,11 +668,10 @@
     activated = (pre / (1.0 + jnp.exp(-pre))).astype(BF16).reshape(tokens, channels)
 
     column = lax.broadcasted_iota(jnp.int32, (tokens, 1), 0) % cols
-    total = conv_acc[1] + dot(activated, conv_w[1, 1])
-    left = pltpu.roll(conv_acc[0] + dot(activated, conv_w[1, 0]), 1, 0)
-    total = total + jnp.where(column == 0, 0.0, left)
-    right = pltpu.roll(conv_acc[2] + dot(activated, conv_w[1, 2]), tokens - 1, 0)
-    total = total + jnp.where(column == cols - 1, 0.0, right)
+    taps = conv_acc[...] + dot(activated, conv_w[1])
+    left, total, right = (taps[:, tap * channels : (tap + 1) * channels] for tap in range(3))
+    total = total + jnp.where(column == 0, 0.0, pltpu.roll(left, 1, 0))
+    total = total + jnp.where(column == cols - 1, 0.0, pltpu.roll(right, tokens - 1, 0))
     total = total.reshape(samples, cols, channels) + conv_bias[...]
     for sample in range(samples):
         out[sample, 0] = (
@@ -705,7 +730,7 @@
             pltpu.VMEM(time_shift.shape, F32),
             pltpu.VMEM(w_qkv.shape, BF16),
             pltpu.VMEM(w_out.shape, BF16),
-            pltpu.VMEM(conv_w.shape, BF16),
+            pltpu.VMEM((3, channels, 3 * channels), BF16),
             pltpu.VMEM((parts, tokens // 4, channels), BF16),
             pltpu.VMEM((2 * cols, channels), BF16),
             pltpu.VMEM((2 * cols, channels), BF16),
@@ -714,7 +739,7 @@
             pltpu.VMEM((2, pairs, 2 * cols), F32),
             pltpu.VMEM((samples + 1, channels, cols), F32),
             pltpu.VMEM((channels, channels), BF16),
-            pltpu.VMEM((3, tokens, channels), F32),
+            pltpu.VMEM((tokens, 3 * channels), F32),
             pltpu.VMEM((n, 2 * samples, channels), F32),
             dma((7,)),
             dma((5,)),

time: 44.7 us -> 39.7 us (0.89)
  Pallas kernels: 43.8 us -> 38.9 us
    pallas_call x1, Pallas kernels: 43.8 us -> 38.9 us  [shards(): pl.pallas_call(functools.partial(kernel, n, plan), out_shape=pltpu.VMEM(h...]
where the time goes in v2:
time: 39.7 us; the launch traced here: 39.6 us
  Pallas kernels  38.9 us (98%)
  local copies, waits for them, and re-layouts  0.73 us (2%)
    pallas_call x1, Pallas kernels, shards(): pl.pallas_call(functools.partial(kernel, n, plan), out_shape=pltpu.VMEM(h...  38.9 us

profile of v2, /device:TPU:0, one launch (start us, length us, event | category | flops | bytes accessed | tf_op | source)
XLA Modules:
  0.0 39.6 jit_solution(7473822367607865062)
XLA Ops:
  0.0 38.9 %section.1 = bf16[2,1,128,640]{3,2,1,0:T(8,128)(2,1)S(1)} custom-call(bf16[256,640]{1,0:T(8,128)(2,1)} %bitcast.3, bf16[4,64,640]{2,1,0:T(8,128)(2,1)} %bitcast.4, bf16[4,64,640]{2,1,0:T(8,128)(2,1)} %bitcast.5, f32[640]{0:T(1024)} %ln_gain_hbm.1, f32[640]{0:T(1024)} %ln_bias_hbm.1, bf16[640,1920]{1,0:T(8,128)(2,1)} %w_qkv_hbm.1, ...), custom_call_target="tpu_custom_call" | custom-call | tf_op jit(solution)/shard_map/section/pallas_call | solution.py:719
  38.9 0.7 %copy.14 = bf16[2,1,128,640]{3,2,1,0:T(8,128)(2,1)} copy(bf16[2,1,128,640]{3,2,1,0:T(8,128)(2,1)S(1)} %section.1) | data formatting | bytes 655360

commit v3 on v2

--- a/solution.py
+++ b/solution.py
@@ -11,6 +11,7 @@
 
 GROUPS = 32
 HEAD_DIM = 64
+LANES = 128
 EPSILON = 1e-05
 MESH = pl.DeviceIdType.MESH
 F32 = jnp.float32
@@ -295,6 +296,8 @@
     soft_far,
     accum,
     same_group,
+    to_group,
+    from_group,
     conv_acc,
     stats,
     load_sem,
@@ -376,11 +379,18 @@
             for at in range(0, len(rows[0]), per)
         ]
 
+        scale = 2**16 // per + 1
+        assert all(i * scale >> 16 == i // per for i in range(len(rows[0])))
+
         def look(i):
-            word = words[0]
-            for k in range(1, len(words)):
-                word = jnp.where(i // per == k, words[k], word)
-            return lax.shift_right_logical(word, i % per * bits) & (2**bits - 1)
+            at = lax.shift_right_logical(i * scale, 16)
+            level, bit = words, 1
+            while len(level) > 1:
+                odd = (at & bit) != 0
+                pairs_of = [level[k : k + 2] for k in range(0, len(level), 2)]
+                level = [jnp.where(odd, p[1], p[0]) if len(p) == 2 else p[0] for p in pairs_of]
+                bit *= 2
+            return lax.shift_right_logical(level[0], (i - at * per) * bits) & (2**bits - 1)
 
         return look
 
@@ -414,12 +424,17 @@
     for load in load_conv:
         load.start()
 
+    def landing_of(part):
+        late = jnp.where(part < q_far, part - 8, jnp.where(part < o_far, part - 12, part - 18))
+        return jnp.where(part < 4 * n, part, late)
+
     def pump(i, carry):
         op = ops(i)
-        part = op // 16
-        landed = jnp.where(part < 4 * n, part, part - 8)
-
-        @pl.when(op // 8 % 2 == 1)
+        part = lax.shift_right_logical(op, 4)
+        stale = part < 4 * n
+        landed = landing_of(part)
+
+        @pl.when((op & 8) != 0)
         def _():
             pltpu.make_async_remote_copy(
                 src_ref=blocks.at[part],
@@ -430,11 +445,11 @@
                 device_id_type=MESH,
             ).wait_recv()
 
-        there = jnp.where(part < 4 * n, part, part + 4)
-        landing = jnp.where(part < 4 * n, part, part - 4)
+        there = jnp.where(stale, part, part + 4)
+        landing = landing_of(there)
         for k, (_, device) in enumerate(neighbours):
 
-            @pl.when(op // 2**k % 2 == 1)
+            @pl.when((op & 2**k) != 0)
             def _(k=k, device=device):
                 pltpu.make_async_remote_copy(
                     src_ref=blocks.at[part],
@@ -484,6 +499,13 @@
     channel_row = lax.broadcasted_iota(jnp.int32, (channels, channels), 0) // group_size
     channel_col = lax.broadcasted_iota(jnp.int32, (channels, channels), 1) // group_size
     same_group[...] = jnp.where(channel_row == channel_col, 1.0, 0.0).astype(BF16)
+    narrow = to_group.shape[1]
+    channel = lax.broadcasted_iota(jnp.int32, (channels, narrow), 0) // group_size
+    group = lax.broadcasted_iota(jnp.int32, (channels, narrow), 1)
+    to_group[...] = jnp.where(channel == group, 1.0, 0.0).astype(BF16)
+    channel = lax.broadcasted_iota(jnp.int32, (narrow, channels), 1) // group_size
+    group = lax.broadcasted_iota(jnp.int32, (narrow, channels), 0)
+    from_group[...] = jnp.where(channel == group, 1.0, 0.0).astype(BF16)
 
     def attend(slot):
         lanes = [slice(pair * 2 * HEAD_DIM, (pair + 1) * 2 * HEAD_DIM) for pair in range(pairs)]
@@ -542,13 +564,13 @@
 
     def step(i, carry):
         code = steps(i)
-        s = code % 2
-        sz = code // 2 % 256
+        s = code & 1
+        sz = lax.shift_right_logical(code, 1) & 255
         first_slot = jnp.where(sz == z, n, 2 * sz + y)
         second_slot = 2 * sz + 1 - y
         low = bounds(i)
         span = bounds(i + 1) - low
-        marks = [low + span * k // 2 for k in range(3)]
+        marks = [low, low + lax.shift_right_logical(span, 1), low + span]
         rows = jnp.concatenate(
             [
                 blocks[pl.ds(slot * 4 + 2 * s, 2)].reshape(cols, channels)
@@ -563,18 +585,18 @@
         attend(s)
         pumps(marks[1], marks[2])
         if MOVED:
-            flag = code // 512
-
-            @pl.when(flag % 2 == 1)
+            flag = lax.shift_right_logical(code, 9)
+
+            @pl.when((flag & 1) != 0)
             def _():
-                @pl.when(flag // 2 % 2 == 1)
+                @pl.when((flag & 2) != 0)
                 def _():
                     far = blocks[q_far : q_far + 2].reshape(cols, channels)
                     spread_queries(samples, far.astype(F32).T.astype(BF16))
 
                 attend(samples)
 
-            @pl.when(flag // 4 % 2 == 1)
+            @pl.when((flag & 4) != 0)
             def _():
                 part = normalised(samples).astype(BF16)
                 blocks[o_own : o_own + 2] = part.reshape(2, cols // 2, channels)
@@ -584,7 +606,7 @@
                         src_ref=blocks.at[o_own + k],
                         dst_ref=blocks.at[o_far + k],
                         send_sem=soft_sem.at[2 + k],
-                        recv_sem=recv_sem.at[o_far + k - 8],
+                        recv_sem=recv_sem.at[4 * n + 10 + k],
                         device_id={"patch": outward},
                         device_id_type=MESH,
                     ).start()
@@ -623,9 +645,7 @@
     square_rows = jnp.concatenate(
         [jnp.sum(centred[s] * centred[s], 0, keepdims=True) for s in range(samples)], 0
     )
-    local_square = split_dot(square_rows, same_group[...])
-    stats[me, :samples] = local_mean
-    stats[me, samples:] = local_square
+    stats[me] = split_dot(jnp.concatenate([sum_rows / cells, square_rows], 0), to_group[...])
 
     def stat_copy(distance):
         return pltpu.make_async_remote_copy(
@@ -663,8 +683,9 @@
     group_mean = jnp.mean(every[:, :samples], 0)
     shift = every[:, :samples] - group_mean[None]
     group_var = (jnp.sum(every[:, samples:], 0) + cells * jnp.sum(shift * shift, 0)) / (cells * n)
-    scale = lax.rsqrt(group_var + EPSILON)
-    pre = (residual - group_mean[:, None, :]) * scale[:, None, :] * gn_gain[...] + gn_bias[...]
+    wide = split_dot(jnp.concatenate([group_mean, lax.rsqrt(group_var + EPSILON)], 0), from_group[...])
+    scale = wide[samples:] * gn_gain[...]
+    pre = (residual - wide[:samples, None, :]) * scale[:, None, :] + gn_bias[...]
     activated = (pre / (1.0 + jnp.exp(-pre))).astype(BF16).reshape(tokens, channels)
 
     column = lax.broadcasted_iota(jnp.int32, (tokens, 1), 0) % cols
@@ -739,12 +760,14 @@
             pltpu.VMEM((2, pairs, 2 * cols), F32),
             pltpu.VMEM((samples + 1, channels, cols), F32),
             pltpu.VMEM((channels, channels), BF16),
+            pltpu.VMEM((channels, LANES), BF16),
+            pltpu.VMEM((LANES, channels), BF16),
             pltpu.VMEM((tokens, 3 * channels), F32),
-            pltpu.VMEM((n, 2 * samples, channels), F32),
+            pltpu.VMEM((n, 2 * samples, LANES), F32),
             dma((7,)),
             dma((5,)),
             dma((3,)),
-            dma((4 * n + (22 if MOVED else 8),)),
+            dma((4 * n + 12,)),
             dma((4,)),
             dma((2,)),
         ],

time: 39.7 us -> 39 us (0.982)
  Pallas kernels: 38.9 us -> 38.1 us
    pallas_call x1, Pallas kernels: 38.9 us -> 38.1 us  [shards(): pl.pallas_call(functools.partial(kernel, n, plan), out_shape=pltpu.VMEM(h...]
where the time goes in v3:
time: 39 us; the launch traced here: 38.8 us
  Pallas kernels  38.1 us (98%)
  local copies, waits for them, and re-layouts  0.73 us (2%)
    pallas_call x1, Pallas kernels, shards(): pl.pallas_call(functools.partial(kernel, n, plan), out_shape=pltpu.VMEM(h...  38.1 us

profile of v3, /device:TPU:0, one launch (start us, length us, event | category | flops | bytes accessed | tf_op | source)
XLA Modules:
  0.0 38.8 jit_solution(8079965139852530382)
XLA Ops:
  0.0 38.1 %section.1 = bf16[2,1,128,640]{3,2,1,0:T(8,128)(2,1)S(1)} custom-call(bf16[256,640]{1,0:T(8,128)(2,1)} %bitcast.3, bf16[4,64,640]{2,1,0:T(8,128)(2,1)} %bitcast.4, bf16[4,64,640]{2,1,0:T(8,128)(2,1)} %bitcast.5, f32[640]{0:T(1024)} %ln_gain_hbm.1, f32[640]{0:T(1024)} %ln_bias_hbm.1, bf16[640,1920]{1,0:T(8,128)(2,1)} %w_qkv_hbm.1, ...), custom_call_target="tpu_custom_call" | custom-call | tf_op jit(solution)/shard_map/section/pallas_call | solution.py:740
  38.1 0.7 %copy.14 = bf16[2,1,128,640]{3,2,1,0:T(8,128)(2,1)} copy(bf16[2,1,128,640]{3,2,1,0:T(8,128)(2,1)S(1)} %section.1) | data formatting | bytes 655360

commit v4 on v3

--- a/solution.py
+++ b/solution.py
@@ -22,32 +22,32 @@
 TUNED = {
     4: [
         (
-            [6, 22, 54, 38, 612, 770, 786, 136, 90, 628, 122, 74, 172, 152, 650, 188, 248, 316, 106, 300, 698, 232, 428, 200, 444, 376, 360, 580, 596, 216, 488, 504, 968, 682, 984, 666],
-            32,
+            [6, 22, 54, 786, 580, 38, 770, 188, 152, 122, 106, 90, 200, 172, 140, 74, 300, 216, 698, 682, 428, 316, 444, 628, 360, 248, 232, 612, 376, 596, 504, 968, 488, 666, 984, 650],
+            33,
             35,
-            [(0, 0, 0), (1, 0, 0), (1, 1, 0), (1, 2, 0), (0, 1, 0), (1, 3, 0)],
-            [12, 19, 22, 27, 30, 32],
+            [(1, 0, 0), (0, 0, 0), (0, 1, 0), (1, 1, 0), (1, 2, 0), (1, 3, 0)],
+            [11, 16, 18, 27, 29, 33],
         ),
         (
-            [135, 151, 167, 10, 268, 284, 26, 201, 183, 42, 313, 396, 58, 217, 328, 234, 250, 840, 412, 297, 580, 856, 628, 429, 344, 596, 88, 445, 472, 456, 72, 120, 360, 104, 666, 612, 376, 650, 712, 488, 682, 504, 698, 760, 744, 728],
-            42,
-            42,
-            [(0, 1, 0), (1, 1, 0), (0, 2, 3), (0, 3, 5), (0, 0, 0), (1, 0, 0), (1, 2, 0), (1, 3, 0)],
-            [14, 17, 25, 30, 31, 34, 37, 42],
+            [135, 151, 183, 268, 10, 26, 201, 167, 58, 284, 297, 328, 412, 217, 396, 42, 596, 580, 429, 840, 250, 234, 856, 313, 344, 120, 456, 612, 445, 472, 104, 504, 682, 72, 488, 760, 376, 744, 628, 88, 650, 666, 360, 698, 728, 712],
+            43,
+            43,
+            [(0, 1, 0), (1, 1, 0), (0, 2, 3), (0, 3, 5), (1, 0, 0), (1, 3, 0), (0, 0, 0), (1, 2, 0)],
+            [14, 22, 25, 30, 31, 35, 40, 43],
         ),
         (
-            [263, 279, 311, 140, 393, 409, 346, 330, 295, 156, 12, 425, 170, 216, 28, 441, 580, 186, 596, 377, 361, 840, 612, 46, 200, 856, 504, 72, 62, 88, 650, 488, 456, 628, 248, 232, 104, 472, 666, 698, 120, 682, 712, 728, 744, 760],
+            [263, 279, 295, 140, 409, 328, 156, 393, 186, 425, 311, 441, 377, 346, 12, 28, 170, 361, 856, 612, 840, 62, 216, 200, 456, 88, 46, 580, 72, 666, 472, 596, 488, 232, 628, 504, 248, 650, 104, 682, 120, 698, 728, 712, 744, 760],
             41,
             41,
-            [(0, 2, 0), (1, 2, 0), (0, 1, 3), (0, 0, 5), (1, 3, 0), (1, 1, 0), (0, 3, 0), (1, 0, 0)],
-            [8, 21, 26, 30, 32, 36, 38, 41],
+            [(0, 2, 0), (1, 2, 0), (0, 1, 3), (0, 0, 5), (0, 3, 0), (1, 3, 0), (1, 1, 0), (1, 0, 0)],
+            [14, 18, 24, 29, 31, 36, 37, 41],
         ),
         (
-            [389, 405, 580, 437, 785, 280, 421, 769, 628, 505, 344, 316, 300, 172, 489, 457, 360, 188, 376, 44, 696, 473, 60, 612, 264, 232, 248, 596, 328, 104, 968, 120, 712, 984, 664, 760, 648, 728, 680, 744],
+            [389, 405, 421, 437, 280, 628, 612, 769, 785, 457, 300, 316, 264, 473, 188, 360, 172, 489, 505, 60, 648, 376, 328, 44, 596, 104, 344, 728, 232, 580, 248, 120, 968, 984, 680, 744, 696, 664, 712, 760],
             32,
             34,
-            [(1, 3, 0), (1, 2, 0), (0, 3, 0), (1, 1, 0), (0, 2, 0), (1, 0, 0)],
-            [15, 19, 22, 27, 29, 32],
+            [(0, 3, 0), (1, 3, 0), (1, 2, 0), (0, 2, 0), (1, 1, 0), (1, 0, 0)],
+            [14, 19, 22, 27, 31, 32],
         ),
     ]
 }
@@ -199,9 +199,9 @@
 
 def device_plan(length):
     n = 2 * length
-    cross = special_parts(length)[1]
+    cross, handed = special_parts(length)[1:3]
     programs = TUNED.get(length) or programs_by_time(length)
-    plan = {name: [] for name in ("ops", "bounds", "steps", "n_steps", "in_loop", "to_merge", "crossed", "n_ops")}
+    plan = {name: [] for name in ("ops", "bounds", "steps", "n_steps", "in_loop", "to_merge", "crossed", "half_handed", "n_ops")}
     plan["sent"] = [[0] * n for _ in range(3)]
     for d in range(n):
         z, y = divmod(d, 2)
@@ -224,6 +224,8 @@
         plan["in_loop"].append(in_loop)
         plan["to_merge"].append(to_merge)
         plan["crossed"].append(max(to_merge, *across))
+        above = [i + 1 for i, code in enumerate(codes) if handed <= code // 16 < handed + 2]
+        plan["half_handed"].append(max(plan["crossed"][-1], *above, 0))
         plan["n_ops"].append(len(ops))
     for name in ("ops", "bounds", "steps"):
         width = max(len(row) for row in plan[name])
@@ -399,6 +401,7 @@
     in_loop = pick(plan["in_loop"])
     to_merge = pick(plan["to_merge"])
     crossed = pick(plan["crossed"])
+    half_handed = pick(plan["half_handed"])
     n_ops = pick(plan["n_ops"])
     soft[...] = jnp.zeros_like(soft)
     for slot in range(samples + 1):
@@ -546,7 +549,7 @@
             row = head * HEAD_DIM
             total = soft[slot, 1, head // 2 : head // 2 + 1, (head % 2) * cols : (head % 2 + 1) * cols]
             accum[slot, row : row + HEAD_DIM] = accum[slot, row : row + HEAD_DIM] * (1.0 / total)
-        return accum[slot].T
+        return accum[slot]
 
     def soft_copy(device):
         return pltpu.make_async_remote_copy(
@@ -598,7 +601,7 @@
 
             @pl.when((flag & 4) != 0)
             def _():
-                part = normalised(samples).astype(BF16)
+                part = normalised(samples).T.astype(BF16)
                 blocks[o_own : o_own + 2] = part.reshape(2, cols // 2, channels)
                 soft_copy(outward).start()
                 for k in range(2):
@@ -633,9 +636,15 @@
                 )
                 soft[(0, 1, *at)] = soft[(0, 1, *at)] * near_scale + far_sum
 
-    attended = jnp.concatenate([normalised(s) for s in range(samples)], 0).astype(BF16)
+    attended = [normalised(s).astype(BF16) for s in range(samples)]
     load_out.wait()
-    residual = hidden[...].astype(F32) + balanced_dot(attended, w_out[...])
+    residual = hidden[...].astype(F32) + jnp.concatenate(
+        [
+            lax.dot_general(a, w_out[...], (((0,), (0,)), ((), ())), preferred_element_type=F32)
+            for a in attended
+        ],
+        0,
+    )
     residual = residual.astype(BF16).astype(F32).reshape(samples, cols, channels)
 
     sum_rows = jnp.concatenate([jnp.sum(residual[s], 0, keepdims=True) for s in range(samples)], 0)
@@ -664,8 +673,11 @@
     pltpu.make_async_copy(conv_w, conv_w, load_sem.at[5]).wait()
     cross_row = jnp.where(y == 0, 2, 0)
     conv_acc[...] = dot(blocks[cross : cross + 4].reshape(tokens, channels), conv_w[cross_row])
-    pumps(crossed, n_ops)
-    conv_acc[...] += dot(blocks[handed : handed + 4].reshape(tokens, channels), conv_w[2 - cross_row])
+    half = tokens // 2
+    for first, last, at in ((crossed, half_handed, 0), (half_handed, n_ops, half)):
+        pumps(first, last)
+        part = blocks[handed + 2 * (at > 0) : handed + 2 * (at > 0) + 2].reshape(half, channels)
+        conv_acc[at : at + half] += dot(part, conv_w[2 - cross_row])
     for load in vectors[2:]:
         load.wait()
     load_shift.wait()

time: 39 us -> 38.4 us (0.985)
  Pallas kernels: 38.1 us -> 37.5 us
    pallas_call x1, Pallas kernels: 38.1 us -> 37.5 us  [shards(): pl.pallas_call(functools.partial(kernel, n, plan), out_shape=pltpu.VMEM(h...]
where the time goes in v4:
time: 38.4 us; the launch traced here: 38.2 us
  Pallas kernels  37.5 us (98%)
  local copies, waits for them, and re-layouts  0.73 us (2%)
    pallas_call x1, Pallas kernels, shards(): pl.pallas_call(functools.partial(kernel, n, plan), out_shape=pltpu.VMEM(h...  37.5 us

profile of v4, /device:TPU:0, one launch (start us, length us, event | category | flops | bytes accessed | tf_op | source)
XLA Modules:
  0.0 38.2 jit_solution(2780849457156497547)
XLA Ops:
  0.0 37.5 %section.1 = bf16[2,1,128,640]{3,2,1,0:T(8,128)(2,1)S(1)} custom-call(bf16[256,640]{1,0:T(8,128)(2,1)} %bitcast.3, bf16[4,64,640]{2,1,0:T(8,128)(2,1)} %bitcast.4, bf16[4,64,640]{2,1,0:T(8,128)(2,1)} %bitcast.5, f32[640]{0:T(1024)} %ln_gain_hbm.1, f32[640]{0:T(1024)} %ln_bias_hbm.1, bf16[640,1920]{1,0:T(8,128)(2,1)} %w_qkv_hbm.1, ...), custom_call_target="tpu_custom_call" | custom-call | tf_op jit(solution)/shard_map/section/pallas_call | solution.py:752
  37.5 0.7 %copy.14 = bf16[2,1,128,640]{3,2,1,0:T(8,128)(2,1)} copy(bf16[2,1,128,640]{3,2,1,0:T(8,128)(2,1)S(1)} %section.1) | data formatting | bytes 655360

commit v5 on v4

--- a/solution.py
+++ b/solution.py
@@ -321,17 +321,6 @@
     y = me % 2
     above_exists = z > 0
     below_exists = z < length - 1
-    neighbours = ((above_exists, me - 2), (below_exists, me + 2), (True, z * 2 + 1 - y))
-
-    barrier = pltpu.get_barrier_semaphore()
-    for there, device in neighbours:
-        def announce(device=device):
-            pl.semaphore_signal(barrier, inc=1, device_id={"patch": device}, device_id_type=MESH)
-        if there is True:
-            announce()
-        else:
-            pl.when(there)(announce)
-
     load_stale = pltpu.make_async_copy(stale_attn_hbm, stale_attn, load_sem.at[0])
     load_hidden = pltpu.make_async_copy(hidden_hbm, hidden, load_sem.at[1])
     load_qkv = pltpu.make_async_copy(w_qkv_hbm, w_qkv, load_sem.at[2])
@@ -362,6 +351,18 @@
     load_stale.start()
     for load in vectors[:2]:
         load.start()
+
+    neighbours = ((above_exists, me - 2), (below_exists, me + 2), (True, z * 2 + 1 - y))
+
+    barrier = pltpu.get_barrier_semaphore()
+    for there, device in neighbours:
+        def announce(device=device):
+            pl.semaphore_signal(barrier, inc=1, device_id={"patch": device}, device_id_type=MESH)
+        if there is True:
+            announce()
+        else:
+            pl.when(there)(announce)
+
     load_hidden.start()
 
     def pick(choices):
@@ -676,8 +677,13 @@
     half = tokens // 2
     for first, last, at in ((crossed, half_handed, 0), (half_handed, n_ops, half)):
         pumps(first, last)
-        part = blocks[handed + 2 * (at > 0) : handed + 2 * (at > 0) + 2].reshape(half, channels)
-        conv_acc[at : at + half] += dot(part, conv_w[2 - cross_row])
+
+        @pl.when(jnp.where(y == 0, above_exists, below_exists))
+        def _(at=at):
+            first_part = handed + at // (half // 2)
+            part = blocks[first_part : first_part + 2].reshape(half, channels)
+            conv_acc[at : at + half] += dot(part, conv_w[2 - cross_row])
+
     for load in vectors[2:]:
         load.wait()
     load_shift.wait()

time: 38.4 us -> 38.4 us (level)
  no operation moved by 1% of the time
where the time goes in v5:
time: 38.4 us; the launch traced here: 38.2 us
  Pallas kernels  37.5 us (98%)
  local copies, waits for them, and re-layouts  0.73 us (2%)
    pallas_call x1, Pallas kernels, shards(): pl.pallas_call(functools.partial(kernel, n, plan), out_shape=pltpu.VMEM(h...  37.5 us

profile of v5, /device:TPU:0, one launch (start us, length us, event | category | flops | bytes accessed | tf_op | source)
XLA Modules:
  0.0 38.2 jit_solution(3368121407203346190)
XLA Ops:
  0.0 37.5 %section.1 = bf16[2,1,128,640]{3,2,1,0:T(8,128)(2,1)S(1)} custom-call(bf16[256,640]{1,0:T(8,128)(2,1)} %bitcast.3, bf16[4,64,640]{2,1,0:T(8,128)(2,1)} %bitcast.4, bf16[4,64,640]{2,1,0:T(8,128)(2,1)} %bitcast.5, f32[640]{0:T(1024)} %ln_gain_hbm.1, f32[640]{0:T(1024)} %ln_bias_hbm.1, bf16[640,1920]{1,0:T(8,128)(2,1)} %w_qkv_hbm.1, ...), custom_call_target="tpu_custom_call" | custom-call | tf_op jit(solution)/shard_map/section/pallas_call | solution.py:758
  37.5 0.7 %copy.14 = bf16[2,1,128,640]{3,2,1,0:T(8,128)(2,1)} copy(bf16[2,1,128,640]{3,2,1,0:T(8,128)(2,1)S(1)} %section.1) | data formatting | bytes 655360

commit v6 on v4

--- a/solution.py
+++ b/solution.py
@@ -301,6 +301,7 @@
     to_group,
     from_group,
     conv_acc,
+    base,
     stats,
     load_sem,
     vector_sem,
@@ -414,7 +415,6 @@
         blocks[handed : handed + 4] = jnp.zeros_like(blocks[handed : handed + 4])
 
     mine = me * 4
-    per_sample = 2
     for load in vectors[:2]:
         load.wait()
     load_stale.wait()
@@ -472,9 +472,11 @@
         part = layer_norm(stale_attn[2 * s : 2 * s + 2], ln_gain[...], ln_bias[...])
         blocks[pl.ds(mine + 2 * s, 2)] = part
 
-    norm_stale(0)
-    pl.semaphore_wait(barrier, 1 + above_exists.astype(jnp.int32) + below_exists.astype(jnp.int32))
-    pumps(0, 2)
+    for half in range(2):
+        blocks[mine + half] = layer_norm(stale_attn[half], ln_gain[...], ln_bias[...])
+        if half == 0:
+            pl.semaphore_wait(barrier, 1 + above_exists.astype(jnp.int32) + below_exists.astype(jnp.int32))
+        pumps(half, half + 1)
     for s in range(1, samples):
         norm_stale(s)
 
@@ -682,6 +684,16 @@
         load.wait()
     load_shift.wait()
 
+    column = lax.broadcasted_iota(jnp.int32, (tokens, 1), 0) % cols
+
+    def shifted(taps):
+        left, middle, right = (taps[:, tap * channels : (tap + 1) * channels] for tap in range(3))
+        middle = middle + jnp.where(column == 0, 0.0, pltpu.roll(left, 1, 0))
+        return middle + jnp.where(column == cols - 1, 0.0, pltpu.roll(right, tokens - 1, 0))
+
+    added = residual + (conv_bias[...] + time_shift[...])[:, None, :]
+    base[...] = shifted(conv_acc[...]) + added.reshape(tokens, channels)
+
     others = stats.at[pl.ds(0, n - 1)]
     pltpu.make_async_remote_copy(
         src_ref=others,
@@ -700,16 +712,8 @@
     pre = (residual - wide[:samples, None, :]) * scale[:, None, :] + gn_bias[...]
     activated = (pre / (1.0 + jnp.exp(-pre))).astype(BF16).reshape(tokens, channels)
 
-    column = lax.broadcasted_iota(jnp.int32, (tokens, 1), 0) % cols
-    taps = conv_acc[...] + dot(activated, conv_w[1])
-    left, total, right = (taps[:, tap * channels : (tap + 1) * channels] for tap in range(3))
-    total = total + jnp.where(column == 0, 0.0, pltpu.roll(left, 1, 0))
-    total = total + jnp.where(column == cols - 1, 0.0, pltpu.roll(right, tokens - 1, 0))
-    total = total.reshape(samples, cols, channels) + conv_bias[...]
-    for sample in range(samples):
-        out[sample, 0] = (
-            total[sample] + time_shift[sample : sample + 1] + residual[sample]
-        ).astype(BF16)
+    total = base[...] + shifted(dot(activated, conv_w[1]))
+    out[:, 0] = total.astype(BF16).reshape(samples, cols, channels)
 
     def sent(source, semaphore):
         pltpu.make_async_remote_copy(
@@ -775,6 +779,7 @@
             pltpu.VMEM((channels, LANES), BF16),
             pltpu.VMEM((LANES, channels), BF16),
             pltpu.VMEM((tokens, 3 * channels), F32),
+            pltpu.VMEM((tokens, channels), F32),
             pltpu.VMEM((n, 2 * samples, LANES), F32),
             dma((7,)),
             dma((5,)),

time: 38.4 us -> 38.3 us (level)
  no operation moved by 1% of the time
where the time goes in v6:
time: 38.3 us; the launch traced here: 38.2 us
  Pallas kernels  37.4 us (98%)
  local copies, waits for them, and re-layouts  0.73 us (2%)
    pallas_call x1, Pallas kernels, shards(): pl.pallas_call(functools.partial(kernel, n, plan), out_shape=pltpu.VMEM(h...  37.4 us

profile of v6, /device:TPU:0, one launch (start us, length us, event | category | flops | bytes accessed | tf_op | source)
XLA Modules:
  0.0 38.2 jit_solution(10895332938901421913)
XLA Ops:
  0.0 37.4 %section.1 = bf16[2,1,128,640]{3,2,1,0:T(8,128)(2,1)S(1)} custom-call(bf16[256,640]{1,0:T(8,128)(2,1)} %bitcast.3, bf16[4,64,640]{2,1,0:T(8,128)(2,1)} %bitcast.4, bf16[4,64,640]{2,1,0:T(8,128)(2,1)} %bitcast.5, f32[640]{0:T(1024)} %ln_gain_hbm.1, f32[640]{0:T(1024)} %ln_bias_hbm.1, bf16[640,1920]{1,0:T(8,128)(2,1)} %w_qkv_hbm.1, ...), custom_call_target="tpu_custom_call" | custom-call | tf_op jit(solution)/shard_map/section/pallas_call | solution.py:756
  37.5 0.7 %copy.14 = bf16[2,1,128,640]{3,2,1,0:T(8,128)(2,1)} copy(bf16[2,1,128,640]{3,2,1,0:T(8,128)(2,1)S(1)} %section.1) | data formatting | bytes 655360
